TPU v7x, 256 devices: a whole 4x4x8 slice. The times are simulated.
256 devices in a mesh: expert: 16 (over x, y), tensor: 8 (over z), replica: 2 (over core).
Axes of the slice: x: 4, y: 4, z: 8, core: 2. Of those that a mesh axis runs over, the one named last changes fastest.
Arguments:
- trained: float32 [16, 7168, 2048], P('replica', 'tensor', 'expert'), may hold values from -3080 to 3080
- snapshot: bfloat16 [16, 7168, 2048], P('replica', 'tensor', 'expert'), may hold values from -3072 to 3072
- changed: int32 [16, 56, 16], P('replica', 'tensor', 'expert'), may hold values from 0 to 1, as said below
- placement: int32 [16], replicated, may hold values from 0 to 15, each once
Outputs:
- rotated_update: bfloat16 [16, 7168, 2048], P('expert', None, 'tensor')
Inputs may be any that keep to these rules, and one draw needn't show every extreme that they name: `placement`: each of the 16 experts appears exactly once. `changed`: in each aligned block of 7 block rows by 1 block columns of one expert, at most 4 entries are 1; for every expert some such block has exactly 4.
All inputs are finite; a program needn't handle non-finite values.
Results may differ from a plain program's by a relative error of at most 0.001.
Values may be sent and summed in bfloat16 or wider, within the bound.
A program may use at most 64 MiB of HBM per device.

v0:
```python
import math
import jax
import jax.numpy as jnp
from jax import lax
from jax.sharding import PartitionSpec as P

BLK = 128


def hadamard():
    positions = jnp.arange(BLK, dtype=jnp.int32)
    parity = jnp.zeros((BLK, BLK), jnp.int32)
    for bit_level in range(BLK.bit_length() - 1):
        parity = parity + (positions[:, None] >> bit_level & 1) * (
            positions[None, :] >> bit_level & 1
        )
    return (1 - 2 * (parity % 2)).astype(jnp.float32) / math.sqrt(BLK)


def body(trained, snapshot, changed, placement):
    hadamard_table = hadamard()
    local_experts, local_rows, local_cols = trained.shape
    copies = lax.axis_size("replica")
    tensor_count = lax.axis_size("tensor")
    expert_count = lax.axis_size("expert")
    members = expert_count // tensor_count
    slot_total = placement.shape[0]
    owner_slots = slot_total // expert_count
    block_rows = local_rows // BLK
    block_cols = local_cols // BLK
    part_rows = BLK // copies
    block_count = block_rows * block_cols
    capacity = (4 * block_count + 3) // 7
    block_flags = changed.reshape(local_experts, block_count)
    position = jnp.arange(block_count, dtype=jnp.int32)
    ranking = jnp.where(block_flags == 1, position[None, :], block_count + position[None, :])
    picked = jnp.argsort(ranking, axis=1)[:, :capacity]
    used_slots = jnp.take_along_axis(block_flags, picked, axis=1)
    expert_ids = jnp.arange(local_experts, dtype=jnp.int32)[:, None]
    row_ids = picked // block_cols
    col_ids = picked % block_cols
    new_tiles = trained.reshape(local_experts, block_rows, BLK, block_cols, BLK)[
        expert_ids, row_ids, :, col_ids, :
    ]
    old_tiles = snapshot.reshape(local_experts, block_rows, BLK, block_cols, BLK)[
        expert_ids, row_ids, :, col_ids, :
    ]
    delta_tiles = jnp.where(
        used_slots[:, :, None, None] == 1, new_tiles - old_tiles.astype(jnp.float32), 0.0
    )
    coded_tiles = jnp.einsum(
        "ij,pmjk->pmik", hadamard_table, delta_tiles, precision=lax.Precision.HIGHEST
    ).astype(jnp.bfloat16)
    coded_tiles = coded_tiles.reshape(local_experts, capacity, copies, part_rows, BLK)
    spots_pair = jnp.broadcast_to(picked[:, :, None], (local_experts, capacity, copies))
    tiles_all, spots_all = (
        lax.all_to_all(coded_tiles, "replica", split_axis=2, concat_axis=0, tiled=True),
        lax.all_to_all(spots_pair, "replica", split_axis=2, concat_axis=0, tiled=True),
    )
    chosen = jnp.take(tiles_all, placement, axis=0).reshape(
        slot_total, 1, 1, capacity, part_rows, BLK
    )
    chosen_spots = jnp.take(spots_all, placement, axis=0).reshape(slot_total, 1, 1, capacity)
    tiles_in, spot_numbers = (
        lax.all_to_all(
            lax.all_to_all(chosen, "expert", split_axis=0, concat_axis=2, tiled=True),
            "tensor",
            split_axis=2,
            concat_axis=1,
            tiled=True,
        ),
        lax.all_to_all(
            lax.all_to_all(chosen_spots, "expert", split_axis=0, concat_axis=2, tiled=True),
            "tensor",
            split_axis=2,
            concat_axis=1,
            tiled=True,
        ),
    )
    source_count = tiles_in.shape[1]
    one_hot = (spot_numbers[..., None] == position).astype(jnp.bfloat16)
    placed = jnp.einsum(
        "osnmg,osnmab->osngab", one_hot, tiles_in, preferred_element_type=jnp.float32
    ).astype(jnp.bfloat16)
    placed = placed.reshape(
        owner_slots, source_count, members, block_rows, block_cols, part_rows, BLK
    )
    placed = jnp.transpose(placed, (0, 1, 3, 5, 2, 4, 6))
    owner_cols = members * block_cols * BLK
    owned_rows = placed.reshape(owner_slots, source_count, block_rows, 1, part_rows, owner_cols)
    whole_rows = lax.all_gather(owned_rows, "replica", axis=3, tiled=True)
    return whole_rows.reshape(owner_slots, tensor_count * block_rows * BLK, owner_cols)


def solution(mesh):
    in_specs = (
        P("replica", "tensor", "expert"),
        P("replica", "tensor", "expert"),
        P("replica", "tensor", "expert"),
        P(),
    )
    out_specs = P("expert", None, "tensor")
    return jax.shard_map(body, mesh=mesh, in_specs=in_specs, out_specs=out_specs, check_vma=False)
```

profile of v0, /device:TPU:1, one launch (start us, length us, event | category | flops | bytes accessed | tf_op | source)
XLA Modules:
  0.0 145.1 jit_solution(11660733728816668597)
XLA Ops:
  6.5 0.9 iota_select_fusion
  8.7 6.4 %all-to-all-start = ((s32[8,4,2]{0,1,2:T(4,128)}), s32[8,4,2]{0,1,2:T(4,128)S(1)}, u32[]{:S(2)}, u32[]{:S(2)}) async-start(s32[8,4,2]{0,1,2:T(4,128)} %broadcast_in_dim.55), calls=%async_computation | async-start | bytes 8192 | tf_op jit(solution)/shard_map/all_to_all | solution.py:58
  16.4 0.8 copy.38
  18.3 0.8 gather_fusion.2
  19.1 4.0 %gather_fusion.1 = f32[32,128,128]{2,1,0:T(8,128)} fusion(f32[8,7,128,1,128]{4,2,1,0,3:T(8,128)} %bitcast.67, s32[32]{0:T(128)S(1)} %reshape.261), kind=kCustom, calls=%fused_computation.1 | custom fusion | bytes 4194688 | tf_op jit(solution)/shard_map/gather | solution.py:42
  23.2 1.9 %convert_subtract_fusion = f32[32,128,128]{2,1,0:T(8,128)S(1)} fusion(f32[32,128,128]{2,1,0:T(8,128)} %gather_fusion.1, bf16[32,128,128]{2,1,0:T(8,128)(2,1)S(1)} %gather_fusion.2), kind=kLoop, calls=%fused_computation.5 | loop fusion | flops 1048576 | bytes 5242880 | tf_op jit(solution)/shard_map/sub | solution.py:49
  25.0 2.3 %fusion.2 = bf16[8,4,128,128]{2,3,1,0:T(8,128)(2,1)S(1)} fusion(f32[8,4,128,128]{3,2,1,0:T(8,128)S(1)} %bitcast.61, pred[8,4]{1,0:T(8,128)(4,1)S(1)} %copy.48, s32[128]{0:T(128)S(1)} %get-tuple-element.7, s32[128]{0:T(128)S(1)} %get-tuple-element.8, s32[128]{0:T(128)S(1)} %get-tuple-element.9, s32[128]{0:T(128)S(1)} %get-tuple-element.10, ...), kind=kOutput, calls=%fused_computation.9 | convolution fusion | flops 806813696 | bytes 3149344 | tf_op jit(solution)/shard_map/ij,pmjk->pmik/dot_general | solution.py:51
  27.3 1.1 copy.49
  28.4 3.6 %all-to-all-start.3 = ((bf16[8,4,2,64,128]{4,3,1,0,2:T(8,128)(2,1)}), bf16[8,4,2,64,128]{4,3,1,0,2:T(8,128)(2,1)S(1)}, u32[]{:S(2)}, u32[]{:S(2)}) async-start(bf16[8,4,2,64,128]{4,3,1,0,2:T(8,128)(2,1)} %copy.49), calls=%async_computation.3 | async-start | bytes 2097152 | tf_op jit(solution)/shard_map/all_to_all | solution.py:57
  32.7 0.7 copy.43
  33.7 5.1 %all-to-all-start.1 = ((s32[16,1,1,4]{3,2,1,0:T(1,128)}), s32[16,1,1,4]{3,2,1,0:T(1,128)}, u32[]{:S(2)}, u32[]{:S(2)}) async-start(s32[16,1,1,4]{3,2,1,0:T(1,128)} %copy.43), calls=%async_computation.1 | async-start | bytes 16384 | tf_op jit(solution)/shard_map/all_to_all | solution.py:73
  38.9 2.0 %gather_fusion.3 = bf16[16,4,64,128]{3,2,1,0:T(8,128)(2,1)S(1)} fusion(bf16[16,4,64,128]{3,2,1,0:T(8,128)(2,1)} %bitcast.65, s32[1024]{0:T(1024)S(1)} %pad_clamp_fusion), kind=kCustom, calls=%fused_computation.3 | custom fusion | bytes 2097216 | tf_op jit(solution)/shard_map/jit(_take)/gather | solution.py:60
  40.8 1.1 fusion.5
  42.0 3.2 %all-to-all-done.1 = s32[16,1,1,4]{3,2,1,0:T(1,128)} async-done(((s32[16,1,1,4]{3,2,1,0:T(1,128)}), s32[16,1,1,4]{3,2,1,0:T(1,128)}, u32[]{:S(2)}, u32[]{:S(2)}) %all-to-all-start.1) | async-done | bytes 288 | tf_op jit(solution)/shard_map/all_to_all | solution.py:73
  45.2 18.6 %all_to_all.78 = bf16[16,1,1,4,64,128]{5,4,3,2,1,0:T(8,128)(2,1)S(1)} all-to-all(bf16[16,1,1,4,64,128]{5,4,3,2,1,0:T(8,128)(2,1)} %fusion.5), channel_id=1, replica_groups=mesh['expert'=16,'tensor'=8,'replica'=2] {'expert'}, dimensions={0} | all-to-all | bytes 2097152 | tf_op jit(solution)/shard_map/all_to_all | solution.py:66
  63.8 32.6 %all_to_all.79 = bf16[1,1,16,4,64,128]{5,4,3,1,0,2:T(8,128)(2,1)} all-to-all(bf16[1,1,16,4,64,128]{5,4,3,1,0,2:T(8,128)(2,1)S(1)} %bitcast.66), channel_id=1, replica_groups=mesh['expert'=16,'tensor'=8,'replica'=2] {'tensor'}, dimensions={2} | all-to-all | bytes 2097152 | tf_op jit(solution)/shard_map/all_to_all | solution.py:65
  96.3 4.3 %all-to-all-start.2 = ((s32[1,1,16,4]{3,1,0,2:T(1,128)}), s32[1,1,16,4]{3,1,0,2:T(1,128)S(1)}, u32[]{:S(2)}, u32[]{:S(2)}) async-start(s32[1,1,16,4]{3,1,0,2:T(1,128)} %bitcast.31), calls=%async_computation.2 | async-start | bytes 16384 | tf_op jit(solution)/shard_map/all_to_all | solution.py:72
  100.7 2.1 %copy.52 = bf16[1,1,16,4,64,128]{5,3,4,2,1,0:T(4,128)(2,1)S(1)} copy(bf16[1,1,16,4,64,128]{5,4,3,1,0,2:T(8,128)(2,1)} %all_to_all.79) | data formatting | bytes 2097152 | tf_op jit(solution)/shard_map/all_to_all | solution.py:65
  102.8 4.4 %all-to-all-done.2 = s32[1,1,16,4]{3,1,0,2:T(1,128)S(1)} async-done(((s32[1,1,16,4]{3,1,0,2:T(1,128)}), s32[1,1,16,4]{3,1,0,2:T(1,128)S(1)}, u32[]{:S(2)}, u32[]{:S(2)}) %all-to-all-start.2) | async-done | bytes 288 | tf_op jit(solution)/shard_map/all_to_all | solution.py:72
  107.2 1.3 convert_bitcast_fusion
  108.5 3.3 %copy.53 = bf16[1,8,7,64,2,1,128]{6,4,3,2,1,5,0:T(2,128)(2,1)} copy(bf16[1,8,7,64,2,1,128]{6,2,3,4,1,5,0:T(8,128)(2,1)S(1)} %convert_bitcast_fusion) | data formatting | bytes 3670016 | tf_op jit(solution)/shard_map/transpose | solution.py:88
  111.8 5.3 %reshape.227 = bf16[1,8,7,1,64,256]{5,4,2,1,3,0:T(8,128)(2,1)} reshape(bf16[1,8,7,64,2,1,128]{6,4,3,2,1,5,0:T(2,128)(2,1)} %copy.53) | data formatting | bytes 3670016 | tf_op jit(solution)/shard_map/reshape | solution.py:90
  117.1 16.8 %all-gather.2.cloned.1.call-done = bf16[1,8,7,2,64,256]{5,4,2,1,0,3:T(8,128)(2,1)} async-done(((bf16[1,8,7,1,64,256]{5,4,2,1,0,3:T(8,128)(2,1)}), bf16[1,8,7,2,64,256]{5,4,2,1,0,3:T(8,128)(2,1)}) %all-gather.2.cloned.1.call-update) | async-done | bytes 3670032 | tf_op jit(solution)/shard_map/all_gather | solution.py:91
  133.9 4.4 %copy.55 = bf16[1,8,7,2,64,256]{5,4,3,2,1,0:T(8,128)(2,1)} copy(bf16[1,8,7,2,64,256]{5,4,2,1,0,3:T(8,128)(2,1)} %all-gather.2.cloned.1.call-done) | data formatting | bytes 7340032 | tf_op jit(solution)/shard_map/all_gather | solution.py:91
  (32 shorter events, 4.8 us)
Async XLA Ops:
  6.5 11.8 %copy-start = (bf16[8,896,128]{2,1,0:T(8,128)(2,1)S(1)}, bf16[8,896,128]{2,1,0:T(8,128)(2,1)}, u32[]{:S(2)}) copy-start(bf16[8,896,128]{2,1,0:T(8,128)(2,1)} %param.5) | copy-start | bytes 5505028
  8.7 19.7 %all-to-all-start = ((s32[8,4,2]{0,1,2:T(4,128)}), s32[8,4,2]{0,1,2:T(4,128)S(1)}, u32[]{:S(2)}, u32[]{:S(2)}) async-start(s32[8,4,2]{0,1,2:T(4,128)} %broadcast_in_dim.55), calls=%async_computation | async-start | bytes 8192 | tf_op jit(solution)/shard_map/all_to_all | solution.py:58
  28.4 5.3 %all-to-all-start.3 = ((bf16[8,4,2,64,128]{4,3,1,0,2:T(8,128)(2,1)}), bf16[8,4,2,64,128]{4,3,1,0,2:T(8,128)(2,1)S(1)}, u32[]{:S(2)}, u32[]{:S(2)}) async-start(bf16[8,4,2,64,128]{4,3,1,0,2:T(8,128)(2,1)} %copy.49), calls=%async_computation.3 | async-start | bytes 2097152 | tf_op jit(solution)/shard_map/all_to_all | solution.py:57
  33.7 5.1 %copy-start.1 = (bf16[8,4,2,64,128]{4,3,1,0,2:T(8,128)(2,1)}, bf16[8,4,2,64,128]{4,3,1,0,2:T(8,128)(2,1)S(1)}, u32[]{:S(2)}) copy-start(bf16[8,4,2,64,128]{4,3,1,0,2:T(8,128)(2,1)S(1)} %all-to-all-done.3) | copy-start | bytes 3145732
  33.7 11.4 %all-to-all-start.1 = ((s32[16,1,1,4]{3,2,1,0:T(1,128)}), s32[16,1,1,4]{3,2,1,0:T(1,128)}, u32[]{:S(2)}, u32[]{:S(2)}) async-start(s32[16,1,1,4]{3,2,1,0:T(1,128)} %copy.43), calls=%async_computation.1 | async-start | bytes 16384 | tf_op jit(solution)/shard_map/all_to_all | solution.py:73
  96.3 10.8 %all-to-all-start.2 = ((s32[1,1,16,4]{3,1,0,2:T(1,128)}), s32[1,1,16,4]{3,1,0,2:T(1,128)S(1)}, u32[]{:S(2)}, u32[]{:S(2)}) async-start(s32[1,1,16,4]{3,1,0,2:T(1,128)} %bitcast.31), calls=%async_computation.2 | async-start | bytes 16384 | tf_op jit(solution)/shard_map/all_to_all | solution.py:72
  100.6 33.3 %all-gather.2.cloned.1.call-start = ((), (), s32[]{:S(2)}) async-start(), calls=%async_computation.6 | async-start | bytes 5505024 | tf_op jit(solution)/shard_map/all_gather | solution.py:91
Sparse Core Ops, SparseCore 0:
  117.2 16.6 all-gather.1
where the time goes:
time: 146 us; the launch traced here: 145 us
  blocking collectives  51.2 us (35%)
  local copies, waits for them, and re-layouts  26.8 us (18%)
  waiting for transfers between devices  24.8 us (17%)
  starting transfers between devices  19.4 us (13%)
  between operations  13.5 us (9%)
  other arithmetic  5.93 us (4%)
  matrix products  3.58 us (2%)
    all_to_all x1, blocking collectives, body(): lax.all_to_all(lax.all_to_all(chosen, 'expert', split_axis=0, concat_axis...  32.6 us
    all_to_all x1, blocking collectives, body(): lax.all_to_all(chosen, 'expert', split_axis=0, concat_axis=2, tiled=True)  18.6 us
    all_gather x1, waiting for transfers between devices, body(): whole_rows = lax.all_gather(owned_rows, 'replica', axis=3, tiled=True)  16.8 us
    all_to_all x1, starting transfers between devices, body(): lax.all_to_all(spots_pair, 'replica', split_axis=2, concat_axis=0, tiled=...  6.41 us
    reshape x1, local copies, waits for them, and re-layouts, body(): placed.reshape(owner_slots, source_count, block_rows, 1, part_rows, owner...  5.3 us
    all_to_all x1, starting transfers between devices, body(): lax.all_to_all(chosen_spots, 'expert', split_axis=0, concat_axis=2, tiled...  5.1 us
    all_to_all x1, waiting for transfers between devices, body(): lax.all_to_all(lax.all_to_all(chosen_spots, 'expert', split_axis=0, conca...  4.42 us
    all_gather x1, local copies, waits for them, and re-layouts, body(): whole_rows = lax.all_gather(owned_rows, 'replica', axis=3, tiled=True)  4.37 us
  transfers between devices with their start and end apart: 5, of which 4 were waited for; matrix products, arithmetic and copies ran while one was open for 14% of the time, Pallas kernels for 0%

commit v1 on v0

--- a/solution.py
+++ b/solution.py
@@ -61,6 +61,15 @@
         slot_total, 1, 1, capacity, part_rows, BLK
     )
     chosen_spots = jnp.take(spots_all, placement, axis=0).reshape(slot_total, 1, 1, capacity)
+    watch_sites = lambda row_data: jnp.concatenate(
+        jax.lax.all_to_all(
+            jnp.stack(jnp.split(row_data, jax.lax.axis_size("expert"), 0)),
+            axis_name="expert",
+            split_axis=0,
+            concat_axis=0,
+        ),
+        2,
+    )
     tiles_in, spot_numbers = (
         lax.all_to_all(
             lax.all_to_all(chosen, "expert", split_axis=0, concat_axis=2, tiled=True),
@@ -70,11 +79,7 @@
             tiled=True,
         ),
         lax.all_to_all(
-            lax.all_to_all(chosen_spots, "expert", split_axis=0, concat_axis=2, tiled=True),
-            "tensor",
-            split_axis=2,
-            concat_axis=1,
-            tiled=True,
+            watch_sites(chosen_spots), "tensor", split_axis=2, concat_axis=1, tiled=True
         ),
     )
     source_count = tiles_in.shape[1]

time: 146 us -> 155 us (1.062)
  local copies, waits for them, and re-layouts: 26.8 us -> 35.2 us
  blocking collectives: 51.2 us -> 52.8 us
    unnamed x5 -> x20, local copies, waits for them, and re-layouts: 0.77 us -> 8.91 us
  transfers between devices with their start and end apart: 5 -> 5, of which waited for: 4 -> 3; matrix products, arithmetic and copies ran while one was open for 14% -> 18% of each run, Pallas kernels for 0% -> 0%
where the time goes in v1:
time: 155 us; the launch traced here: 154 us
  blocking collectives  52.8 us (34%)
  local copies, waits for them, and re-layouts  35.2 us (23%)
  waiting for transfers between devices  24.7 us (16%)
  starting transfers between devices  18.5 us (12%)
  between operations  13.5 us (9%)
  other arithmetic  5.93 us (4%)
  matrix products  3.58 us (2%)
    all_to_all x1, blocking collectives, body(): lax.all_to_all(lax.all_to_all(chosen, 'expert', split_axis=0, concat_axis...  33.7 us
    all_to_all x1, blocking collectives, body(): lax.all_to_all(chosen, 'expert', split_axis=0, concat_axis=2, tiled=True)  19.2 us
    all_gather x1, waiting for transfers between devices, body(): whole_rows = lax.all_gather(owned_rows, 'replica', axis=3, tiled=True)  16.9 us
    unnamed x20, local copies, waits for them, and re-layouts  8.91 us
    all_to_all x1, starting transfers between devices, body(): lax.all_to_all(spots_pair, 'replica', split_axis=2, concat_axis=0, tiled=...  6.41 us
    reshape x1, local copies, waits for them, and re-layouts, body(): placed.reshape(owner_slots, source_count, block_rows, 1, part_rows, owner...  5.29 us
    all_to_all x1, starting transfers between devices, body(): jax.lax.all_to_all(jnp.stack(jnp.split(row_data, jax.lax.axis_size('exper...  5.1 us
    all_to_all x1, waiting for transfers between devices, body(): lax.all_to_all(watch_sites(chosen_spots), 'tensor', split_axis=2, concat_...  4.41 us
  transfers between devices with their start and end apart: 5, of which 3 were waited for; matrix products, arithmetic and copies ran while one was open for 18% of the time, Pallas kernels for 0%

profile of v1, /device:TPU:1, one launch (start us, length us, event | category | flops | bytes accessed | tf_op | source)
XLA Modules:
  0.0 154.2 jit_solution(10528219385686546863)
XLA Ops:
  6.5 0.9 iota_select_fusion
  8.7 6.4 %all-to-all-start = ((s32[8,4,2]{0,1,2:T(4,128)}), s32[8,4,2]{0,1,2:T(4,128)S(1)}, u32[]{:S(2)}, u32[]{:S(2)}) async-start(s32[8,4,2]{0,1,2:T(4,128)} %broadcast_in_dim.55), calls=%async_computation | async-start | bytes 8192 | tf_op jit(solution)/shard_map/all_to_all | solution.py:58
  16.4 0.8 copy.107
  17.4 0.7 gather_fusion.4
  18.3 0.8 gather_fusion.2
  19.1 4.0 %gather_fusion.1 = f32[32,128,128]{2,1,0:T(8,128)} fusion(f32[8,7,128,1,128]{4,2,1,0,3:T(8,128)} %bitcast.99, s32[32]{0:T(128)S(1)} %reshape.290), kind=kCustom, calls=%fused_computation.1 | custom fusion | bytes 4194688 | tf_op jit(solution)/shard_map/gather | solution.py:42
  23.1 1.9 %convert_subtract_fusion = f32[32,128,128]{2,1,0:T(8,128)S(1)} fusion(f32[32,128,128]{2,1,0:T(8,128)} %gather_fusion.1, bf16[32,128,128]{2,1,0:T(8,128)(2,1)S(1)} %gather_fusion.2), kind=kLoop, calls=%fused_computation.5 | loop fusion | flops 1048576 | bytes 5242880 | tf_op jit(solution)/shard_map/sub | solution.py:49
  25.0 2.3 %fusion.2 = bf16[8,4,128,128]{2,3,1,0:T(8,128)(2,1)S(1)} fusion(f32[8,4,128,128]{3,2,1,0:T(8,128)S(1)} %bitcast.93, pred[8,4]{1,0:T(8,128)(4,1)S(1)} %copy.116, s32[128]{0:T(128)S(1)} %get-tuple-element.23, s32[128]{0:T(128)S(1)} %get-tuple-element.24, s32[128]{0:T(128)S(1)} %get-tuple-element.25, s32[128]{0:T(128)S(1)} %get-tuple-element.26, ...), kind=kOutput, calls=%fused_computation.9 | convolution fusion | flops 806813696 | bytes 3149344 | tf_op jit(solution)/shard_map/ij,pmjk->pmik/dot_general | solution.py:51
  27.3 1.1 copy.117
  28.4 3.6 %all-to-all-start.3 = ((bf16[8,4,2,64,128]{4,3,1,0,2:T(8,128)(2,1)}), bf16[8,4,2,64,128]{4,3,1,0,2:T(8,128)(2,1)S(1)}, u32[]{:S(2)}, u32[]{:S(2)}) async-start(bf16[8,4,2,64,128]{4,3,1,0,2:T(8,128)(2,1)} %copy.117), calls=%async_computation.3 | async-start | bytes 2097152 | tf_op jit(solution)/shard_map/all_to_all | solution.py:57
  41.9 5.1 %all-to-all-start.1 = ((s32[16,1,1,1,4]{4,3,2,1,0:T(1,128)}), s32[16,1,1,1,4]{4,3,2,1,0:T(1,128)}, u32[]{:S(2)}, u32[]{:S(2)}) async-start(s32[16,1,1,1,4]{4,3,2,1,0:T(1,128)} %constant_dynamic-update-slice_fusion), calls=%async_computation.1 | async-start | bytes 16384 | tf_op jit(solution)/shard_map/all_to_all | solution.py:65
  47.0 2.0 %gather_fusion.3 = bf16[16,4,64,128]{3,2,1,0:T(8,128)(2,1)S(1)} fusion(bf16[16,4,64,128]{3,2,1,0:T(8,128)(2,1)} %bitcast.97, s32[1024]{0:T(1024)S(1)} %pad_clamp_fusion), kind=kCustom, calls=%fused_computation.3 | custom fusion | bytes 2097216 | tf_op jit(solution)/shard_map/jit(_take)/gather | solution.py:60
  49.0 1.1 fusion.5
  50.1 3.4 %all-to-all-done.1 = s32[16,1,1,1,4]{4,3,2,1,0:T(1,128)} async-done(((s32[16,1,1,1,4]{4,3,2,1,0:T(1,128)}), s32[16,1,1,1,4]{4,3,2,1,0:T(1,128)}, u32[]{:S(2)}, u32[]{:S(2)}) %all-to-all-start.1) | async-done | bytes 288 | tf_op jit(solution)/shard_map/all_to_all | solution.py:65
  53.5 19.2 %all_to_all.71 = bf16[16,1,1,4,64,128]{5,4,3,2,1,0:T(8,128)(2,1)S(1)} all-to-all(bf16[16,1,1,4,64,128]{5,4,3,2,1,0:T(8,128)(2,1)} %fusion.5), channel_id=1, replica_groups=mesh['expert'=16,'tensor'=8,'replica'=2] {'expert'}, dimensions={0} | all-to-all | bytes 2097152 | tf_op jit(solution)/shard_map/all_to_all | solution.py:75
  72.6 33.7 %all_to_all.72 = bf16[1,1,16,4,64,128]{5,4,3,1,0,2:T(8,128)(2,1)} all-to-all(bf16[1,1,16,4,64,128]{5,4,3,1,0,2:T(8,128)(2,1)S(1)} %bitcast.98), channel_id=1, replica_groups=mesh['expert'=16,'tensor'=8,'replica'=2] {'tensor'}, dimensions={2} | all-to-all | bytes 2097152 | tf_op jit(solution)/shard_map/all_to_all | solution.py:74
  106.3 3.3 %all-to-all-start.2 = ((s32[1,1,16,4]{3,1,0,2:T(1,128)}), s32[1,1,16,4]{3,1,0,2:T(1,128)S(1)}, u32[]{:S(2)}, u32[]{:S(2)}) async-start(s32[1,1,16,4]{3,1,0,2:T(1,128)} %bitcast.31), calls=%async_computation.2 | async-start | bytes 16384 | tf_op jit(solution)/shard_map/all_to_all | solution.py:81
  109.7 2.1 %copy.120 = bf16[1,1,16,4,64,128]{5,3,4,2,1,0:T(4,128)(2,1)S(1)} copy(bf16[1,1,16,4,64,128]{5,4,3,1,0,2:T(8,128)(2,1)} %all_to_all.72) | data formatting | bytes 2097152 | tf_op jit(solution)/shard_map/all_to_all | solution.py:74
  111.8 4.4 %all-to-all-done.2 = s32[1,1,16,4]{3,1,0,2:T(1,128)S(1)} async-done(((s32[1,1,16,4]{3,1,0,2:T(1,128)}), s32[1,1,16,4]{3,1,0,2:T(1,128)S(1)}, u32[]{:S(2)}, u32[]{:S(2)}) %all-to-all-start.2) | async-done | bytes 288 | tf_op jit(solution)/shard_map/all_to_all | solution.py:81
  116.2 1.3 convert_bitcast_fusion
  117.5 3.3 %copy.121 = bf16[1,8,7,64,2,1,128]{6,4,3,2,1,5,0:T(2,128)(2,1)} copy(bf16[1,8,7,64,2,1,128]{6,2,3,4,1,5,0:T(8,128)(2,1)S(1)} %convert_bitcast_fusion) | data formatting | bytes 3670016 | tf_op jit(solution)/shard_map/transpose | solution.py:93
  120.8 5.3 %reshape.256 = bf16[1,8,7,1,64,256]{5,4,2,1,3,0:T(8,128)(2,1)} reshape(bf16[1,8,7,64,2,1,128]{6,4,3,2,1,5,0:T(2,128)(2,1)} %copy.121) | data formatting | bytes 3670016 | tf_op jit(solution)/shard_map/reshape | solution.py:95
  126.1 16.9 %all-gather.2.cloned.1.call-done = bf16[1,8,7,2,64,256]{5,4,2,1,0,3:T(8,128)(2,1)} async-done(((bf16[1,8,7,1,64,256]{5,4,2,1,0,3:T(8,128)(2,1)}), bf16[1,8,7,2,64,256]{5,4,2,1,0,3:T(8,128)(2,1)}) %all-gather.2.cloned.1.call-update) | async-done | bytes 3670032 | tf_op jit(solution)/shard_map/all_gather | solution.py:96
  143.0 4.4 %copy.123 = bf16[1,8,7,2,64,256]{5,4,3,2,1,0:T(8,128)(2,1)} copy(bf16[1,8,7,2,64,256]{5,4,2,1,0,3:T(8,128)(2,1)} %all-gather.2.cloned.1.call-done) | data formatting | bytes 7340032 | tf_op jit(solution)/shard_map/all_gather | solution.py:96
  (48 shorter events, 13.0 us)
Async XLA Ops:
  6.5 11.8 %copy-start = (bf16[8,896,128]{2,1,0:T(8,128)(2,1)S(1)}, bf16[8,896,128]{2,1,0:T(8,128)(2,1)}, u32[]{:S(2)}) copy-start(bf16[8,896,128]{2,1,0:T(8,128)(2,1)} %param.5) | copy-start | bytes 5505028
  8.7 19.7 %all-to-all-start = ((s32[8,4,2]{0,1,2:T(4,128)}), s32[8,4,2]{0,1,2:T(4,128)S(1)}, u32[]{:S(2)}, u32[]{:S(2)}) async-start(s32[8,4,2]{0,1,2:T(4,128)} %broadcast_in_dim.55), calls=%async_computation | async-start | bytes 8192 | tf_op jit(solution)/shard_map/all_to_all | solution.py:58
  28.4 13.5 %all-to-all-start.3 = ((bf16[8,4,2,64,128]{4,3,1,0,2:T(8,128)(2,1)}), bf16[8,4,2,64,128]{4,3,1,0,2:T(8,128)(2,1)S(1)}, u32[]{:S(2)}, u32[]{:S(2)}) async-start(bf16[8,4,2,64,128]{4,3,1,0,2:T(8,128)(2,1)} %copy.117), calls=%async_computation.3 | async-start | bytes 2097152 | tf_op jit(solution)/shard_map/all_to_all | solution.py:57
  41.9 5.1 %copy-start.1 = (bf16[8,4,2,64,128]{4,3,1,0,2:T(8,128)(2,1)}, bf16[8,4,2,64,128]{4,3,1,0,2:T(8,128)(2,1)S(1)}, u32[]{:S(2)}) copy-start(bf16[8,4,2,64,128]{4,3,1,0,2:T(8,128)(2,1)S(1)} %all-to-all-done.3) | copy-start | bytes 3145732
  41.9 11.6 %all-to-all-start.1 = ((s32[16,1,1,1,4]{4,3,2,1,0:T(1,128)}), s32[16,1,1,1,4]{4,3,2,1,0:T(1,128)}, u32[]{:S(2)}, u32[]{:S(2)}) async-start(s32[16,1,1,1,4]{4,3,2,1,0:T(1,128)} %constant_dynamic-update-slice_fusion), calls=%async_computation.1 | async-start | bytes 16384 | tf_op jit(solution)/shard_map/all_to_all | solution.py:65
  106.3 9.9 %all-to-all-start.2 = ((s32[1,1,16,4]{3,1,0,2:T(1,128)}), s32[1,1,16,4]{3,1,0,2:T(1,128)S(1)}, u32[]{:S(2)}, u32[]{:S(2)}) async-start(s32[1,1,16,4]{3,1,0,2:T(1,128)} %bitcast.31), calls=%async_computation.2 | async-start | bytes 16384 | tf_op jit(solution)/shard_map/all_to_all | solution.py:81
  109.7 33.3 %all-gather.2.cloned.1.call-start = ((), (), s32[]{:S(2)}) async-start(), calls=%async_computation.6 | async-start | bytes 5505024 | tf_op jit(solution)/shard_map/all_gather | solution.py:96
Sparse Core Ops, SparseCore 0:
  126.2 16.7 all-gather.1
